TPU v7x, 32 devices: a whole 2x2x4 slice. The times are simulated.
32 devices in a mesh: farcp: 2 (over x), nearcp: 4 (over y, core), model: 4 (over z).
Axes of the slice: x: 2, y: 2, z: 4, core: 2. Of those that a mesh axis runs over, the one named last changes fastest.
Arguments:
- raw_keys: bfloat16 [8, 8192, 8, 128], P(None, ('farcp', 'nearcp'), 'model'), may hold values from -6 to 6
- raw_values: bfloat16 [8, 8192, 8, 128], P(None, ('farcp', 'nearcp'), 'model'), may hold values from -6 to 6
- turn_angle: float32 [8192, 64], replicated, may hold values from -3.140625 to 3.140625
- key_gain: float32 [128], replicated, may hold values from 0.25 to 1.75
Outputs:
- stored_keys: bfloat16 [8, 8192, 8, 128], P(('farcp', 'nearcp'), None, 'model')
- stored_values: bfloat16 [8, 8192, 8, 128], P(('farcp', 'nearcp'), None, 'model')
- key_scale: float32 [8, 8, 128], P(('farcp', 'nearcp'), 'model')
All inputs are finite; a program needn't handle non-finite values. Where the computation divides by a largest or mean magnitude, that divisor is 1e-20 or more.
Results may differ from a plain program's by a relative error of at most 0.001.
Values may be sent and summed in bfloat16 or wider, within the bound.
No kernel may reach another device: no remote copies, remote signals or barrier semaphores. Data moves between devices by JAX's collectives and lax.ppermute only.
A program may use at most 192 MiB of HBM per device.

v0:
```python
import functools

import jax
import jax.numpy as jnp
from jax import lax
from jax.experimental import pallas as pl
from jax.experimental.pallas import tpu as pltpu
from jax.sharding import PartitionSpec as P


GROUP = ("farcp", "nearcp")
TILE = 128
UNROLL = 2


def partner(me, step, count):
    return me ^ step if count & (count - 1) == 0 else (me + step) % count


def sender(me, step, count):
    return me ^ step if count & (count - 1) == 0 else (me + count - step) % count


def orders(count):
    def hops(step):
        return bin(step >> 1).count("1")

    steps = range(1, count)
    keys = sorted(steps, key=lambda step: (step < 2, step & 1, -hops(step), step))
    values = sorted(steps, key=lambda step: (hops(step), step & 1, -step))
    return tuple(keys), tuple(values)


def in_hbm(array):
    return pltpu.with_memory_space_constraint(array, pltpu.HBM)


def cut_kernel(count, steps, whole, *refs):
    pieces, sems = refs[: len(steps)], refs[len(steps)]
    me = lax.axis_index(GROUP)
    copies = [
        pltpu.make_async_copy(whole.at[partner(me, step, count)], piece, sems.at[slot])
        for slot, (step, piece) in enumerate(zip(steps, pieces))
    ]
    for copy in copies:
        copy.start()
    for copy in copies:
        copy.wait()


def cut(whole, steps):
    count, rows, lanes = whole.shape
    return pl.pallas_call(
        functools.partial(cut_kernel, count, steps),
        out_shape=[pltpu.VMEM((rows, lanes), whole.dtype)] * len(steps),
        in_specs=[pl.BlockSpec(memory_space=pltpu.HBM)],
        out_specs=[pl.BlockSpec(memory_space=pltpu.VMEM)] * len(steps),
        scratch_shapes=[pltpu.SemaphoreType.DMA((len(steps),))],
        compiler_params=pltpu.CompilerParams(vmem_limit_bytes=8 << 20),
    )(in_hbm(whole))


def exchange(pieces, steps, count):
    moved = []
    for step, piece in zip(steps, pieces):
        pairs = [(source, int(partner(source, step, count))) for source in range(count)]
        moved.append(lax.ppermute(piece, GROUP, pairs))
    return moved


def table_kernel(heads, angle, cosine, sine):
    turn = angle[...]
    c, s = jnp.cos(turn), jnp.sin(turn)
    c = jnp.concatenate([c, c], axis=0).T
    s = jnp.concatenate([-s, s], axis=0).T
    for head in range(heads):
        at = pl.ds(head, c.shape[0], stride=heads)
        cosine[at, :] = c
        sine[at, :] = s


def tables(turn_angle, heads, block=512):
    length, half = turn_angle.shape
    shape = pltpu.HBM((length * heads, 2 * half), jnp.float32)
    return pl.pallas_call(
        functools.partial(table_kernel, heads),
        out_shape=[shape, shape],
        grid=(length // block,),
        in_specs=[pl.BlockSpec((half, block), lambda i: (0, i))],
        out_specs=[pl.BlockSpec((block * heads, 2 * half), lambda i: (i, 0))] * 2,
        compiler_params=pltpu.CompilerParams(vmem_limit_bytes=8 << 20),
        cost_estimate=pl.CostEstimate(flops=length * half * 400, bytes_accessed=length * half * 40, transcendentals=0),
    )(in_hbm(turn_angle.T))


def keys_kernel(count, heads, steps, own, *refs):
    number = len(steps)
    pieces = refs[:number]
    cosine, sine, gain, stored, scale = refs[number : number + 5]
    block, turned, cos_in, sin_in, out, in_sems, tab_sems, out_sems = refs[number + 5 :]
    rows, lanes = block.shape
    half = lanes // 2
    me = lax.axis_index(GROUP)
    sources = [me] + [sender(me, step, count) for step in steps]
    first = pltpu.make_async_copy(own.at[me], block, in_sems)
    first.start()

    def fetch(slot):
        part = pl.ds(sources[slot] * rows, rows)
        return (
            pltpu.make_async_copy(cosine.at[part], cos_in.at[slot % 2], tab_sems.at[slot % 2, 0]),
            pltpu.make_async_copy(sine.at[part], sin_in.at[slot % 2], tab_sems.at[slot % 2, 1]),
        )

    for copy in fetch(0):
        copy.start()
    first.wait()
    peak = jnp.zeros((8, lanes), jnp.float32)
    factor = gain[...]
    for slot in range(number + 1):
        piece = block if slot == 0 else pieces[slot - 1]
        for copy in fetch(slot):
            copy.wait()
        if slot < number:
            for copy in fetch(slot + 1):
                copy.start()

        def turn(index, peak, slot=slot, piece=piece):
            part = pl.ds(pl.multiple_of(index * TILE, TILE), TILE)
            wide = piece[part, :].astype(jnp.float32)
            mean = jnp.sum(wide * wide, axis=-1, keepdims=True) * (1.0 / lanes)
            wide = wide * lax.rsqrt(mean + 1e-06) * factor
            wide = wide * cos_in[slot % 2, part, :] + pltpu.roll(wide, half, 1) * sin_in[slot % 2, part, :]
            turned[slot, part, :] = wide
            return jnp.maximum(peak, jnp.max(jnp.abs(wide).reshape(TILE // 8, 8, lanes), axis=0))

        peak = lax.fori_loop(0, rows // TILE, turn, peak, unroll=UNROLL)
    tops = [peak[head : head + 1] for head in range(heads)]
    for row in range(heads, 8):
        tops[row % heads] = jnp.maximum(tops[row % heads], peak[row : row + 1])
    top = jnp.concatenate(tops, axis=0)
    scale[...] = top
    inverse = 1.0 / jnp.concatenate([top] * (8 // heads), axis=0)
    for slot in range(number + 1):
        copy = pltpu.make_async_copy(
            out.at[slot % 2], stored.at[pl.ds(sources[slot] * rows, rows)], out_sems.at[slot % 2]
        )
        if slot >= 2:
            copy.wait()

        def narrow(index, carry, slot=slot):
            part = pl.ds(pl.multiple_of(index * TILE, TILE), TILE)
            wide = turned[slot, part, :].reshape(TILE // 8, 8, lanes) * inverse[None]
            out[slot % 2, part, :] = wide.reshape(TILE, lanes).astype(out.dtype)
            return carry

        lax.fori_loop(0, rows // TILE, narrow, 0, unroll=UNROLL)
        copy.start()
    for slot in range(max(number - 1, 0), number + 1):
        pltpu.make_async_copy(
            out.at[slot % 2], stored.at[pl.ds(sources[slot] * rows, rows)], out_sems.at[slot % 2]
        ).wait()


def finish_keys(own, pieces, cosine, sine, gain, steps, heads):
    count, rows, lanes = own.shape
    return pl.pallas_call(
        functools.partial(keys_kernel, count, heads, steps),
        out_shape=[
            jax.ShapeDtypeStruct((count * rows, lanes), own.dtype),
            jax.ShapeDtypeStruct((heads, lanes), jnp.float32),
        ],
        in_specs=[pl.BlockSpec(memory_space=pltpu.HBM)]
        + [pl.BlockSpec(memory_space=pltpu.VMEM)] * len(pieces)
        + [pl.BlockSpec(memory_space=pltpu.HBM)] * 2
        + [pl.BlockSpec(memory_space=pltpu.VMEM)],
        out_specs=[pl.BlockSpec(memory_space=pltpu.HBM), pl.BlockSpec(memory_space=pltpu.VMEM)],
        scratch_shapes=[
            pltpu.VMEM((rows, lanes), own.dtype),
            pltpu.VMEM((count, rows, lanes), jnp.float32),
            pltpu.VMEM((2, rows, lanes), jnp.float32),
            pltpu.VMEM((2, rows, lanes), jnp.float32),
            pltpu.VMEM((2, rows, lanes), own.dtype),
            pltpu.SemaphoreType.DMA,
            pltpu.SemaphoreType.DMA((2, 2)),
            pltpu.SemaphoreType.DMA((2,)),
        ],
        compiler_params=pltpu.CompilerParams(vmem_limit_bytes=24 << 20),
        cost_estimate=pl.CostEstimate(flops=count * rows * lanes * 200, bytes_accessed=count * rows * lanes * 8, transcendentals=0),
    )(in_hbm(own), *pieces, in_hbm(cosine), in_hbm(sine), gain)


def place_kernel(count, steps, own, *refs):
    number = len(steps)
    if own:
        local, refs = refs[1], refs[2:]
    else:
        refs = refs[1:]
    pieces, whole = refs[:number], refs[number]
    rows = whole.shape[0] // count
    me = lax.axis_index(GROUP)
    if own:
        block, in_sem, sems = refs[number + 1 :]
        first = pltpu.make_async_copy(local.at[me], block, in_sem)
        first.start()
    else:
        sems = refs[number + 1]
    copies = [
        pltpu.make_async_copy(piece, whole.at[pl.ds(sender(me, step, count) * rows, rows)], sems.at[slot])
        for slot, (step, piece) in enumerate(zip(steps, pieces))
    ]
    for copy in copies:
        copy.start()
    if own:
        first.wait()
        last = pltpu.make_async_copy(block, whole.at[pl.ds(me * rows, rows)], in_sem)
        last.start()
        last.wait()
    for copy in copies:
        copy.wait()


def place(before, own, pieces, steps, count):
    rows, lanes = pieces[0].shape
    number = len(steps)
    scratch = [pltpu.SemaphoreType.DMA((number,))]
    operands = [in_hbm(before)]
    if own is not None:
        operands.append(in_hbm(own))
        scratch = [pltpu.VMEM((rows, lanes), own.dtype), pltpu.SemaphoreType.DMA] + scratch
    return pl.pallas_call(
        functools.partial(place_kernel, count, steps, own is not None),
        out_shape=pltpu.HBM((count * rows, lanes), pieces[0].dtype),
        in_specs=[pl.BlockSpec(memory_space=pltpu.HBM)] * len(operands)
        + [pl.BlockSpec(memory_space=pltpu.VMEM)] * number,
        out_specs=pl.BlockSpec(memory_space=pltpu.HBM),
        scratch_shapes=scratch,
        input_output_aliases={} if own is not None else {0: 0},
        compiler_params=pltpu.CompilerParams(vmem_limit_bytes=4 << 20),
    )(*operands, *pieces)


def local(raw_keys, raw_values, turn_angle, key_gain):
    count, length, heads, lanes = raw_keys.shape
    rows = length * heads
    keys = raw_keys.reshape(count, rows, lanes)
    values = raw_values.reshape(count, rows, lanes)
    steps, value_steps = orders(count)
    early = cut(keys, steps[:1])
    early += cut(keys, steps[1:])
    late = cut(values, value_steps)
    key_pieces = exchange(early, steps, count)
    value_pieces = exchange(late, value_steps, count)
    cosine, sine = tables(turn_angle, heads)
    stored_keys, key_scale = finish_keys(keys, key_pieces, cosine, sine, key_gain.reshape(1, lanes), steps, heads)
    arrived = dict(zip(value_steps, value_pieces))
    stored_values, own = key_scale, values
    for group in (value_steps[:-3], value_steps[-3:-2], value_steps[-2:-1], value_steps[-1:]):
        if not group:
            continue
        stored_values = place(stored_values, own, [arrived[step] for step in group], group, count)
        own = None
    whole = (1, count * length, heads, lanes)
    return stored_keys.reshape(whole), stored_values.reshape(whole), key_scale[None]


def solution(mesh):
    in_specs = (
        P(None, GROUP, "model", None),
        P(None, GROUP, "model", None),
        P(),
        P(),
    )
    out_specs = (
        P(GROUP, None, "model", None),
        P(GROUP, None, "model", None),
        P(GROUP, "model", None),
    )
    return jax.shard_map(local, mesh=mesh, in_specs=in_specs, out_specs=out_specs, check_vma=False)
```

profile of v0, /device:TPU:0, one launch (start us, length us, event | category | flops | bytes accessed | tf_op | source)
XLA Modules:
  0.0 106.9 jit_solution(15900927456640084723)
XLA Ops:
  0.6 1.9 %shard_map.68 = (bf16[2048,128]{1,0:T(8,128)(2,1)S(1)}, bf16[2048,128]{1,0:T(8,128)(2,1)S(1)}, bf16[2048,128]{1,0:T(8,128)(2,1)S(1)}, bf16[2048,128]{1,0:T(8,128...) custom-call(bf16[8,2048,128]{2,1,0:T(8,128)(2,1)} %bitcast.9), custom_call_target="tpu_custom_call" | custom-call | tf_op jit(solution)/shard_map/pallas_call | solution.py:53
  2.5 3.1 %collective-permute-start.1 = (bf16[2048,128]{1,0:T(8,128)(2,1)S(1)}, bf16[2048,128]{1,0:T(8,128)(2,1)S(1)}, u32[]{:S(2)}, u32[]{:S(2)}) collective-permute-start(bf16[2048,128]{1,0:T(8,128)(2,1)S(1)} %get-tuple-element.20), channel_id=1, source_target_pairs={{0,8},{4,12},{8,0},{12,4},{16,24},{20,28},{24,16},{28,20},{1,9},{5... | collective-permute-start | bytes 1572872 | tf_op jit(solution)/shard_map/ppermute | solution.py:67
  5.6 1.5 %collective-permute-start.2 = (bf16[2048,128]{1,0:T(8,128)(2,1)S(1)}, bf16[2048,128]{1,0:T(8,128)(2,1)S(1)}, u32[]{:S(2)}, u32[]{:S(2)}) collective-permute-start(bf16[2048,128]{1,0:T(8,128)(2,1)S(1)} %get-tuple-element.21), channel_id=1, source_target_pairs={{0,16},{4,20},{8,24},{12,28},{16,0},{20,4},{24,8},{28,12},{1,17},{... | collective-permute-start | bytes 1572872 | tf_op jit(solution)/shard_map/ppermute | solution.py:67
  7.1 1.7 %collective-permute-start.4 = (bf16[2048,128]{1,0:T(8,128)(2,1)S(1)}, bf16[2048,128]{1,0:T(8,128)(2,1)S(1)}, u32[]{:S(2)}, u32[]{:S(2)}) collective-permute-start(bf16[2048,128]{1,0:T(8,128)(2,1)S(1)} %get-tuple-element.23), channel_id=1, source_target_pairs={{0,12},{4,8},{8,4},{12,0},{16,28},{20,24},{24,20},{28,16},{1,13},{... | collective-permute-start | bytes 1572872 | tf_op jit(solution)/shard_map/ppermute | solution.py:67
  9.2 1.0 shard_map.67
  10.2 8.8 %collective-permute-done.1.refs_1_ = bf16[2048,128]{1,0:T(8,128)(2,1)S(1)} collective-permute-done((bf16[2048,128]{1,0:T(8,128)(2,1)S(1)}, bf16[2048,128]{1,0:T(8,128)(2,1)S(1)}, u32[]{:S(2)}, u32[]{:S(2)}) %collective-permute-start.1) | collective-permute-done | bytes 524320 | tf_op jit(solution)/shard_map/ppermute | solution.py:67
  19.1 2.0 %shard_map.71 = (bf16[2048,128]{1,0:T(8,128)(2,1)S(1)}, bf16[2048,128]{1,0:T(8,128)(2,1)S(1)}, bf16[2048,128]{1,0:T(8,128)(2,1)S(1)}, bf16[2048,128]{1,0:T(8,128...) custom-call(bf16[8,2048,128]{2,1,0:T(8,128)(2,1)} %bitcast.12), custom_call_target="tpu_custom_call" | custom-call | tf_op jit(solution)/shard_map/pallas_call | solution.py:53
  21.2 3.6 %collective-permute-start = (bf16[2048,128]{1,0:T(8,128)(2,1)S(1)}, bf16[2048,128]{1,0:T(8,128)(2,1)S(1)}, u32[]{:S(2)}, u32[]{:S(2)}) collective-permute-start(bf16[2048,128]{1,0:T(8,128)(2,1)S(1)} %shard_map.67), channel_id=1, source_target_pairs={{0,24},{4,28},{8,16},{12,20},{16,8},{20,12},{24,0},{28,4},{1,25},{... | collective-permute-start | bytes 1572872 | tf_op jit(solution)/shard_map/ppermute | solution.py:67
  24.8 5.9 %collective-permute-done.3.refs_3_ = bf16[2048,128]{1,0:T(8,128)(2,1)S(1)} collective-permute-done((bf16[2048,128]{1,0:T(8,128)(2,1)S(1)}, bf16[2048,128]{1,0:T(8,128)(2,1)S(1)}, u32[]{:S(2)}, u32[]{:S(2)}) %collective-permute-start.3) | collective-permute-done | bytes 524320 | tf_op jit(solution)/shard_map/ppermute | solution.py:67
  30.7 1.9 %collective-permute-start.10 = (bf16[2048,128]{1,0:T(8,128)(2,1)S(1)}, bf16[2048,128]{1,0:T(8,128)(2,1)S(1)}, u32[]{:S(2)}, u32[]{:S(2)}) collective-permute-start(bf16[2048,128]{1,0:T(8,128)(2,1)S(1)} %get-tuple-element.33), channel_id=1, source_target_pairs={{0,20},{4,16},{8,28},{12,24},{16,4},{20,0},{24,12},{28,8},{1,21},{... | collective-permute-start | bytes 1572872 | tf_op jit(solution)/shard_map/ppermute | solution.py:67
  32.5 6.8 %collective-permute-done.4.refs_4_ = bf16[2048,128]{1,0:T(8,128)(2,1)S(1)} collective-permute-done((bf16[2048,128]{1,0:T(8,128)(2,1)S(1)}, bf16[2048,128]{1,0:T(8,128)(2,1)S(1)}, u32[]{:S(2)}, u32[]{:S(2)}) %collective-permute-start.4) | collective-permute-done | bytes 524320 | tf_op jit(solution)/shard_map/ppermute | solution.py:67
  39.3 0.8 collective-permute-start.7
  40.1 1.8 %collective-permute-done.5.refs_5_ = bf16[2048,128]{1,0:T(8,128)(2,1)S(1)} collective-permute-done((bf16[2048,128]{1,0:T(8,128)(2,1)S(1)}, bf16[2048,128]{1,0:T(8,128)(2,1)S(1)}, u32[]{:S(2)}, u32[]{:S(2)}) %collective-permute-start.5) | collective-permute-done | bytes 524320 | tf_op jit(solution)/shard_map/ppermute | solution.py:67
  41.9 0.5 collective-permute-start.8
  42.5 0.8 collective-permute-start.9
  43.2 10.5 %collective-permute-done.refs_0_ = bf16[2048,128]{1,0:T(8,128)(2,1)S(1)} collective-permute-done((bf16[2048,128]{1,0:T(8,128)(2,1)S(1)}, bf16[2048,128]{1,0:T(8,128)(2,1)S(1)}, u32[]{:S(2)}, u32[]{:S(2)}) %collective-permute-start) | collective-permute-done | bytes 524320 | tf_op jit(solution)/shard_map/ppermute | solution.py:67
  53.7 10.7 %collective-permute-done.10.refs_5_ = bf16[2048,128]{1,0:T(8,128)(2,1)S(1)} collective-permute-done((bf16[2048,128]{1,0:T(8,128)(2,1)S(1)}, bf16[2048,128]{1,0:T(8,128)(2,1)S(1)}, u32[]{:S(2)}, u32[]{:S(2)}) %collective-permute-start.10) | collective-permute-done | bytes 524320 | tf_op jit(solution)/shard_map/ppermute | solution.py:67
  64.5 3.3 %collective-permute-start.13 = (bf16[2048,128]{1,0:T(8,128)(2,1)S(1)}, bf16[2048,128]{1,0:T(8,128)(2,1)S(1)}, u32[]{:S(2)}, u32[]{:S(2)}) collective-permute-start(bf16[2048,128]{1,0:T(8,128)(2,1)S(1)} %get-tuple-element.36), channel_id=1, source_target_pairs={{0,28},{4,24},{8,20},{12,16},{16,12},{20,8},{24,4},{28,0},{1,29},{... | collective-permute-start | bytes 1572872 | tf_op jit(solution)/shard_map/ppermute | solution.py:67
  67.8 15.3 %shard_map.69 = (f32[16384,128]{1,0:T(8,128)}, f32[16384,128]{1,0:T(8,128)}) custom-call(f32[64,8192]{1,0:T(8,128)} %bitcast.14), custom_call_target="tpu_custom_call" | custom-call | flops 209715200 | bytes 20971520 | tf_op jit(solution)/shard_map/pallas_call | solution.py:85
  83.1 19.0 %shard_map.70 = (bf16[16384,128]{1,0:T(8,128)(2,1)}, f32[2,128]{1,0:T(2,128)}) custom-call(bf16[8,2048,128]{2,1,0:T(8,128)(2,1)} %bitcast.11, bf16[2048,128]{1,0:T(8,128)(2,1)S(1)} %collective-permute-done.refs_0_, bf16[2048,128]{1,0:T(8,128)(2,1)S(1)} %collective-permute-done.1.refs_1_, bf16[2048,128]{1,0:T(8,128)(2,1)S(1)} %collective-permute-done.2.refs_2_, ...), custom_call_target="tpu_custom_call" | custom-call | flops 419430400 | bytes 16777216 | tf_op jit(solution)/shard_map/pallas_call | solution.py:167
  102.1 2.3 %shard_map.72.refs_0_ = bf16[16384,128]{1,0:T(8,128)(2,1)} custom-call(f32[2,128]{1,0:T(2,128)} %get-tuple-element.29.refs_0_, bf16[8,2048,128]{2,1,0:T(8,128)(2,1)} %bitcast.13, bf16[2048,128]{1,0:T(8,128)(2,1)S(1)} %collective-permute-done.7.refs_2_, bf16[2048,128]{1,0:T(8,128)(2,1)S(1)} %collective-permute-done.8.refs_3_, ...), custom_call_target="tpu_custom_call" | custom-call | tf_op jit(solution)/shard_map/pallas_call | solution.py:231
  104.4 0.8 shard_map.73.refs_0_
  105.2 0.8 shard_map.74.refs_0_
  106.1 0.8 shard_map.75
  (15 shorter events, 0.5 us)
Async XLA Ops:
  2.5 16.6 %collective-permute-start.1 = (bf16[2048,128]{1,0:T(8,128)(2,1)S(1)}, bf16[2048,128]{1,0:T(8,128)(2,1)S(1)}, u32[]{:S(2)}, u32[]{:S(2)}) collective-permute-start(bf16[2048,128]{1,0:T(8,128)(2,1)S(1)} %get-tuple-element.20), channel_id=1, source_target_pairs={{0,8},{4,12},{8,0},{12,4},{16,24},{20,28},{24,16},{28,20},{1,9},{5... | collective-permute-start | bytes 1572872 | tf_op jit(solution)/shard_map/ppermute | solution.py:67
  5.6 15.6 %collective-permute-start.2 = (bf16[2048,128]{1,0:T(8,128)(2,1)S(1)}, bf16[2048,128]{1,0:T(8,128)(2,1)S(1)}, u32[]{:S(2)}, u32[]{:S(2)}) collective-permute-start(bf16[2048,128]{1,0:T(8,128)(2,1)S(1)} %get-tuple-element.21), channel_id=1, source_target_pairs={{0,16},{4,20},{8,24},{12,28},{16,0},{20,4},{24,8},{28,12},{1,17},{... | collective-permute-start | bytes 1572872 | tf_op jit(solution)/shard_map/ppermute | solution.py:67
  7.1 23.6 %collective-permute-start.3 = (bf16[2048,128]{1,0:T(8,128)(2,1)S(1)}, bf16[2048,128]{1,0:T(8,128)(2,1)S(1)}, u32[]{:S(2)}, u32[]{:S(2)}) collective-permute-start(bf16[2048,128]{1,0:T(8,128)(2,1)S(1)} %get-tuple-element.22), channel_id=1, source_target_pairs={{0,28},{4,24},{8,20},{12,16},{16,12},{20,8},{24,4},{28,0},{1,29},{... | collective-permute-start | bytes 1572872 | tf_op jit(solution)/shard_map/ppermute | solution.py:67
  7.1 32.2 %collective-permute-start.4 = (bf16[2048,128]{1,0:T(8,128)(2,1)S(1)}, bf16[2048,128]{1,0:T(8,128)(2,1)S(1)}, u32[]{:S(2)}, u32[]{:S(2)}) collective-permute-start(bf16[2048,128]{1,0:T(8,128)(2,1)S(1)} %get-tuple-element.23), channel_id=1, source_target_pairs={{0,12},{4,8},{8,4},{12,0},{16,28},{20,24},{24,20},{28,16},{1,13},{... | collective-permute-start | bytes 1572872 | tf_op jit(solution)/shard_map/ppermute | solution.py:67
  8.8 33.1 %collective-permute-start.5 = (bf16[2048,128]{1,0:T(8,128)(2,1)S(1)}, bf16[2048,128]{1,0:T(8,128)(2,1)S(1)}, u32[]{:S(2)}, u32[]{:S(2)}) collective-permute-start(bf16[2048,128]{1,0:T(8,128)(2,1)S(1)} %get-tuple-element.24), channel_id=1, source_target_pairs={{0,20},{4,16},{8,28},{12,24},{16,4},{20,0},{24,12},{28,8},{1,21},{... | collective-permute-start | bytes 1572872 | tf_op jit(solution)/shard_map/ppermute | solution.py:67
  10.2 72.9 %copy-start = (f32[128]{0:T(128)S(1)}, f32[128]{0:T(128)}, u32[]{:S(2)}) copy-start(f32[128]{0:T(128)} %param.7) | copy-start | bytes 1540
  19.1 23.4 %collective-permute-start.6 = (bf16[2048,128]{1,0:T(8,128)(2,1)S(1)}, bf16[2048,128]{1,0:T(8,128)(2,1)S(1)}, u32[]{:S(2)}, u32[]{:S(2)}) collective-permute-start(bf16[2048,128]{1,0:T(8,128)(2,1)S(1)} %get-tuple-element.25), channel_id=1, source_target_pairs={{0,4},{4,0},{8,12},{12,8},{16,20},{20,16},{24,28},{28,24},{1,5},{5... | collective-permute-start | bytes 1572872 | tf_op jit(solution)/shard_map/ppermute | solution.py:67
  21.2 32.5 %collective-permute-start = (bf16[2048,128]{1,0:T(8,128)(2,1)S(1)}, bf16[2048,128]{1,0:T(8,128)(2,1)S(1)}, u32[]{:S(2)}, u32[]{:S(2)}) collective-permute-start(bf16[2048,128]{1,0:T(8,128)(2,1)S(1)} %shard_map.67), channel_id=1, source_target_pairs={{0,24},{4,28},{8,16},{12,20},{16,8},{20,12},{24,0},{28,4},{1,25},{... | collective-permute-start | bytes 1572872 | tf_op jit(solution)/shard_map/ppermute | solution.py:67
  30.7 33.7 %collective-permute-start.10 = (bf16[2048,128]{1,0:T(8,128)(2,1)S(1)}, bf16[2048,128]{1,0:T(8,128)(2,1)S(1)}, u32[]{:S(2)}, u32[]{:S(2)}) collective-permute-start(bf16[2048,128]{1,0:T(8,128)(2,1)S(1)} %get-tuple-element.33), channel_id=1, source_target_pairs={{0,20},{4,16},{8,28},{12,24},{16,4},{20,0},{24,12},{28,8},{1,21},{... | collective-permute-start | bytes 1572872 | tf_op jit(solution)/shard_map/ppermute | solution.py:67
  39.3 25.2 %collective-permute-start.7 = (bf16[2048,128]{1,0:T(8,128)(2,1)S(1)}, bf16[2048,128]{1,0:T(8,128)(2,1)S(1)}, u32[]{:S(2)}, u32[]{:S(2)}) collective-permute-start(bf16[2048,128]{1,0:T(8,128)(2,1)S(1)} %get-tuple-element.30), channel_id=1, source_target_pairs={{0,4},{4,0},{8,12},{12,8},{16,20},{20,16},{24,28},{28,24},{1,5},{5... | collective-permute-start | bytes 1572872 | tf_op jit(solution)/shard_map/ppermute | solution.py:67
  41.9 60.2 %collective-permute-start.8 = (bf16[2048,128]{1,0:T(8,128)(2,1)S(1)}, bf16[2048,128]{1,0:T(8,128)(2,1)S(1)}, u32[]{:S(2)}, u32[]{:S(2)}) collective-permute-start(bf16[2048,128]{1,0:T(8,128)(2,1)S(1)} %get-tuple-element.31), channel_id=1, source_target_pairs={{0,16},{4,20},{8,24},{12,28},{16,0},{20,4},{24,8},{28,12},{1,17},{... | collective-permute-start | bytes 1572872 | tf_op jit(solution)/shard_map/ppermute | solution.py:67
  42.5 59.7 %collective-permute-start.9 = (bf16[2048,128]{1,0:T(8,128)(2,1)S(1)}, bf16[2048,128]{1,0:T(8,128)(2,1)S(1)}, u32[]{:S(2)}, u32[]{:S(2)}) collective-permute-start(bf16[2048,128]{1,0:T(8,128)(2,1)S(1)} %get-tuple-element.32), channel_id=1, source_target_pairs={{0,8},{4,12},{8,0},{12,4},{16,24},{20,28},{24,16},{28,20},{1,9},{5... | collective-permute-start | bytes 1572872 | tf_op jit(solution)/shard_map/ppermute | solution.py:67
  53.7 50.7 %collective-permute-start.11 = (bf16[2048,128]{1,0:T(8,128)(2,1)S(1)}, bf16[2048,128]{1,0:T(8,128)(2,1)S(1)}, u32[]{:S(2)}, u32[]{:S(2)}) collective-permute-start(bf16[2048,128]{1,0:T(8,128)(2,1)S(1)} %get-tuple-element.34), channel_id=1, source_target_pairs={{0,12},{4,8},{8,4},{12,0},{16,28},{20,24},{24,20},{28,16},{1,13},{... | collective-permute-start | bytes 1572872 | tf_op jit(solution)/shard_map/ppermute | solution.py:67
  64.4 40.8 %collective-permute-start.12 = (bf16[2048,128]{1,0:T(8,128)(2,1)S(1)}, bf16[2048,128]{1,0:T(8,128)(2,1)S(1)}, u32[]{:S(2)}, u32[]{:S(2)}) collective-permute-start(bf16[2048,128]{1,0:T(8,128)(2,1)S(1)} %get-tuple-element.35), channel_id=1, source_target_pairs={{0,24},{4,28},{8,16},{12,20},{16,8},{20,12},{24,0},{28,4},{1,25},{... | collective-permute-start | bytes 1572872 | tf_op jit(solution)/shard_map/ppermute | solution.py:67
  64.5 41.6 %collective-permute-start.13 = (bf16[2048,128]{1,0:T(8,128)(2,1)S(1)}, bf16[2048,128]{1,0:T(8,128)(2,1)S(1)}, u32[]{:S(2)}, u32[]{:S(2)}) collective-permute-start(bf16[2048,128]{1,0:T(8,128)(2,1)S(1)} %get-tuple-element.36), channel_id=1, source_target_pairs={{0,28},{4,24},{8,20},{12,16},{16,12},{20,8},{24,4},{28,0},{1,29},{... | collective-permute-start | bytes 1572872 | tf_op jit(solution)/shard_map/ppermute | solution.py:67
where the time goes:
time: 107 us
  waiting for transfers between devices  44.5 us (42%)
  Pallas kernels  44 us (41%)
  starting transfers between devices  17.6 us (16%)
    ppermute x14, waiting for transfers between devices, exchange(): moved.append(lax.ppermute(piece, GROUP, pairs))  44.5 us
    pallas_call x1, Pallas kernels, finish_keys(): pl.pallas_call(functools.partial(keys_kernel, count, heads, steps), out_s...  19 us
    ppermute x14, starting transfers between devices, exchange(): moved.append(lax.ppermute(piece, GROUP, pairs))  17.6 us
    pallas_call x1, Pallas kernels, tables(): pl.pallas_call(functools.partial(table_kernel, heads), out_shape=[shape,...  15.3 us
    pallas_call x3, Pallas kernels, cut(): pl.pallas_call(functools.partial(cut_kernel, count, steps), out_shape=[pl...  4.99 us
    pallas_call x4, Pallas kernels, place(): pl.pallas_call(functools.partial(place_kernel, count, steps, own is not N...  4.71 us
  transfers between devices with their start and end apart: 14, of which 6 were waited for; matrix products, arithmetic and copies ran while one was open for 0% of the time, Pallas kernels for 39%

commit v1 on v0

--- a/solution.py
+++ b/solution.py
@@ -11,6 +11,7 @@
 GROUP = ("farcp", "nearcp")
 TILE = 128
 UNROLL = 2
+PARTS = 2
 
 
 def partner(me, step, count):
@@ -205,9 +206,15 @@
         first.start()
     else:
         sems = refs[number + 1]
+    size = rows // PARTS
     copies = [
-        pltpu.make_async_copy(piece, whole.at[pl.ds(sender(me, step, count) * rows, rows)], sems.at[slot])
+        pltpu.make_async_copy(
+            piece.at[pl.ds(part * size, size)],
+            whole.at[pl.ds(sender(me, step, count) * rows + part * size, size)],
+            sems.at[slot, part],
+        )
         for slot, (step, piece) in enumerate(zip(steps, pieces))
+        for part in range(PARTS)
     ]
     for copy in copies:
         copy.start()
@@ -223,7 +230,7 @@
 def place(before, own, pieces, steps, count):
     rows, lanes = pieces[0].shape
     number = len(steps)
-    scratch = [pltpu.SemaphoreType.DMA((number,))]
+    scratch = [pltpu.SemaphoreType.DMA((number, PARTS))]
     operands = [in_hbm(before)]
     if own is not None:
         operands.append(in_hbm(own))

time: 107 us -> 108 us (level)
  no operation moved by 1% of the time
where the time goes in v1:
time: 108 us; the launch traced here: 107 us
  waiting for transfers between devices  44.5 us (41%)
  Pallas kernels  44.1 us (41%)
  starting transfers between devices  17.6 us (16%)
    ppermute x14, waiting for transfers between devices, exchange(): moved.append(lax.ppermute(piece, GROUP, pairs))  44.5 us
    pallas_call x1, Pallas kernels, finish_keys(): pl.pallas_call(functools.partial(keys_kernel, count, heads, steps), out_s...  19 us
    ppermute x14, starting transfers between devices, exchange(): moved.append(lax.ppermute(piece, GROUP, pairs))  17.6 us
    pallas_call x1, Pallas kernels, tables(): pl.pallas_call(functools.partial(table_kernel, heads), out_shape=[shape,...  15.3 us
    pallas_call x3, Pallas kernels, cut(): pl.pallas_call(functools.partial(cut_kernel, count, steps), out_shape=[pl...  4.99 us
    pallas_call x4, Pallas kernels, place(): pl.pallas_call(functools.partial(place_kernel, count, steps, own is not N...  4.8 us
  transfers between devices with their start and end apart: 14, of which 6 were waited for; matrix products, arithmetic and copies ran while one was open for 0% of the time, Pallas kernels for 39%

profile of v1, /device:TPU:0, one launch (start us, length us, event | category | flops | bytes accessed | tf_op | source)
XLA Modules:
  0.0 107.0 jit_solution(7436670578187991941)
XLA Ops:
  0.6 1.9 %shard_map.68 = (bf16[2048,128]{1,0:T(8,128)(2,1)S(1)}, bf16[2048,128]{1,0:T(8,128)(2,1)S(1)}, bf16[2048,128]{1,0:T(8,128)(2,1)S(1)}, bf16[2048,128]{1,0:T(8,128...) custom-call(bf16[8,2048,128]{2,1,0:T(8,128)(2,1)} %bitcast.9), custom_call_target="tpu_custom_call" | custom-call | tf_op jit(solution)/shard_map/pallas_call | solution.py:54
  2.5 3.1 %collective-permute-start.1 = (bf16[2048,128]{1,0:T(8,128)(2,1)S(1)}, bf16[2048,128]{1,0:T(8,128)(2,1)S(1)}, u32[]{:S(2)}, u32[]{:S(2)}) collective-permute-start(bf16[2048,128]{1,0:T(8,128)(2,1)S(1)} %get-tuple-element.20), channel_id=1, source_target_pairs={{0,8},{4,12},{8,0},{12,4},{16,24},{20,28},{24,16},{28,20},{1,9},{5... | collective-permute-start | bytes 1572872 | tf_op jit(solution)/shard_map/ppermute | solution.py:68
  5.6 1.5 %collective-permute-start.2 = (bf16[2048,128]{1,0:T(8,128)(2,1)S(1)}, bf16[2048,128]{1,0:T(8,128)(2,1)S(1)}, u32[]{:S(2)}, u32[]{:S(2)}) collective-permute-start(bf16[2048,128]{1,0:T(8,128)(2,1)S(1)} %get-tuple-element.21), channel_id=1, source_target_pairs={{0,16},{4,20},{8,24},{12,28},{16,0},{20,4},{24,8},{28,12},{1,17},{... | collective-permute-start | bytes 1572872 | tf_op jit(solution)/shard_map/ppermute | solution.py:68
  7.1 1.7 %collective-permute-start.4 = (bf16[2048,128]{1,0:T(8,128)(2,1)S(1)}, bf16[2048,128]{1,0:T(8,128)(2,1)S(1)}, u32[]{:S(2)}, u32[]{:S(2)}) collective-permute-start(bf16[2048,128]{1,0:T(8,128)(2,1)S(1)} %get-tuple-element.23), channel_id=1, source_target_pairs={{0,12},{4,8},{8,4},{12,0},{16,28},{20,24},{24,20},{28,16},{1,13},{... | collective-permute-start | bytes 1572872 | tf_op jit(solution)/shard_map/ppermute | solution.py:68
  9.2 1.0 shard_map.67
  10.2 8.8 %collective-permute-done.1.refs_1_ = bf16[2048,128]{1,0:T(8,128)(2,1)S(1)} collective-permute-done((bf16[2048,128]{1,0:T(8,128)(2,1)S(1)}, bf16[2048,128]{1,0:T(8,128)(2,1)S(1)}, u32[]{:S(2)}, u32[]{:S(2)}) %collective-permute-start.1) | collective-permute-done | bytes 524320 | tf_op jit(solution)/shard_map/ppermute | solution.py:68
  19.1 2.0 %shard_map.71 = (bf16[2048,128]{1,0:T(8,128)(2,1)S(1)}, bf16[2048,128]{1,0:T(8,128)(2,1)S(1)}, bf16[2048,128]{1,0:T(8,128)(2,1)S(1)}, bf16[2048,128]{1,0:T(8,128...) custom-call(bf16[8,2048,128]{2,1,0:T(8,128)(2,1)} %bitcast.12), custom_call_target="tpu_custom_call" | custom-call | tf_op jit(solution)/shard_map/pallas_call | solution.py:54
  21.2 3.6 %collective-permute-start = (bf16[2048,128]{1,0:T(8,128)(2,1)S(1)}, bf16[2048,128]{1,0:T(8,128)(2,1)S(1)}, u32[]{:S(2)}, u32[]{:S(2)}) collective-permute-start(bf16[2048,128]{1,0:T(8,128)(2,1)S(1)} %shard_map.67), channel_id=1, source_target_pairs={{0,24},{4,28},{8,16},{12,20},{16,8},{20,12},{24,0},{28,4},{1,25},{... | collective-permute-start | bytes 1572872 | tf_op jit(solution)/shard_map/ppermute | solution.py:68
  24.8 5.9 %collective-permute-done.3.refs_3_ = bf16[2048,128]{1,0:T(8,128)(2,1)S(1)} collective-permute-done((bf16[2048,128]{1,0:T(8,128)(2,1)S(1)}, bf16[2048,128]{1,0:T(8,128)(2,1)S(1)}, u32[]{:S(2)}, u32[]{:S(2)}) %collective-permute-start.3) | collective-permute-done | bytes 524320 | tf_op jit(solution)/shard_map/ppermute | solution.py:68
  30.7 1.9 %collective-permute-start.10 = (bf16[2048,128]{1,0:T(8,128)(2,1)S(1)}, bf16[2048,128]{1,0:T(8,128)(2,1)S(1)}, u32[]{:S(2)}, u32[]{:S(2)}) collective-permute-start(bf16[2048,128]{1,0:T(8,128)(2,1)S(1)} %get-tuple-element.33), channel_id=1, source_target_pairs={{0,20},{4,16},{8,28},{12,24},{16,4},{20,0},{24,12},{28,8},{1,21},{... | collective-permute-start | bytes 1572872 | tf_op jit(solution)/shard_map/ppermute | solution.py:68
  32.5 6.8 %collective-permute-done.4.refs_4_ = bf16[2048,128]{1,0:T(8,128)(2,1)S(1)} collective-permute-done((bf16[2048,128]{1,0:T(8,128)(2,1)S(1)}, bf16[2048,128]{1,0:T(8,128)(2,1)S(1)}, u32[]{:S(2)}, u32[]{:S(2)}) %collective-permute-start.4) | collective-permute-done | bytes 524320 | tf_op jit(solution)/shard_map/ppermute | solution.py:68
  39.3 0.8 collective-permute-start.7
  40.1 1.8 %collective-permute-done.5.refs_5_ = bf16[2048,128]{1,0:T(8,128)(2,1)S(1)} collective-permute-done((bf16[2048,128]{1,0:T(8,128)(2,1)S(1)}, bf16[2048,128]{1,0:T(8,128)(2,1)S(1)}, u32[]{:S(2)}, u32[]{:S(2)}) %collective-permute-start.5) | collective-permute-done | bytes 524320 | tf_op jit(solution)/shard_map/ppermute | solution.py:68
  41.9 0.5 collective-permute-start.8
  42.5 0.8 collective-permute-start.9
  43.2 10.5 %collective-permute-done.refs_0_ = bf16[2048,128]{1,0:T(8,128)(2,1)S(1)} collective-permute-done((bf16[2048,128]{1,0:T(8,128)(2,1)S(1)}, bf16[2048,128]{1,0:T(8,128)(2,1)S(1)}, u32[]{:S(2)}, u32[]{:S(2)}) %collective-permute-start) | collective-permute-done | bytes 524320 | tf_op jit(solution)/shard_map/ppermute | solution.py:68
  53.7 10.7 %collective-permute-done.10.refs_5_ = bf16[2048,128]{1,0:T(8,128)(2,1)S(1)} collective-permute-done((bf16[2048,128]{1,0:T(8,128)(2,1)S(1)}, bf16[2048,128]{1,0:T(8,128)(2,1)S(1)}, u32[]{:S(2)}, u32[]{:S(2)}) %collective-permute-start.10) | collective-permute-done | bytes 524320 | tf_op jit(solution)/shard_map/ppermute | solution.py:68
  64.5 3.3 %collective-permute-start.13 = (bf16[2048,128]{1,0:T(8,128)(2,1)S(1)}, bf16[2048,128]{1,0:T(8,128)(2,1)S(1)}, u32[]{:S(2)}, u32[]{:S(2)}) collective-permute-start(bf16[2048,128]{1,0:T(8,128)(2,1)S(1)} %get-tuple-element.36), channel_id=1, source_target_pairs={{0,28},{4,24},{8,20},{12,16},{16,12},{20,8},{24,4},{28,0},{1,29},{... | collective-permute-start | bytes 1572872 | tf_op jit(solution)/shard_map/ppermute | solution.py:68
  67.8 15.3 %shard_map.69 = (f32[16384,128]{1,0:T(8,128)}, f32[16384,128]{1,0:T(8,128)}) custom-call(f32[64,8192]{1,0:T(8,128)} %bitcast.14), custom_call_target="tpu_custom_call" | custom-call | flops 209715200 | bytes 20971520 | tf_op jit(solution)/shard_map/pallas_call | solution.py:86
  83.1 19.0 %shard_map.70 = (bf16[16384,128]{1,0:T(8,128)(2,1)}, f32[2,128]{1,0:T(2,128)}) custom-call(bf16[8,2048,128]{2,1,0:T(8,128)(2,1)} %bitcast.11, bf16[2048,128]{1,0:T(8,128)(2,1)S(1)} %collective-permute-done.refs_0_, bf16[2048,128]{1,0:T(8,128)(2,1)S(1)} %collective-permute-done.1.refs_1_, bf16[2048,128]{1,0:T(8,128)(2,1)S(1)} %collective-permute-done.2.refs_2_, ...), custom_call_target="tpu_custom_call" | custom-call | flops 419430400 | bytes 16777216 | tf_op jit(solution)/shard_map/pallas_call | solution.py:168
  102.1 2.3 %shard_map.72.refs_0_ = bf16[16384,128]{1,0:T(8,128)(2,1)} custom-call(f32[2,128]{1,0:T(2,128)} %get-tuple-element.29.refs_0_, bf16[8,2048,128]{2,1,0:T(8,128)(2,1)} %bitcast.13, bf16[2048,128]{1,0:T(8,128)(2,1)S(1)} %collective-permute-done.7.refs_2_, bf16[2048,128]{1,0:T(8,128)(2,1)S(1)} %collective-permute-done.8.refs_3_, ...), custom_call_target="tpu_custom_call" | custom-call | tf_op jit(solution)/shard_map/pallas_call | solution.py:238
  104.5 0.8 shard_map.73.refs_0_
  105.3 0.8 shard_map.74.refs_0_
  106.2 0.8 shard_map.75
  (15 shorter events, 0.5 us)
Async XLA Ops:
  2.5 16.6 %collective-permute-start.1 = (bf16[2048,128]{1,0:T(8,128)(2,1)S(1)}, bf16[2048,128]{1,0:T(8,128)(2,1)S(1)}, u32[]{:S(2)}, u32[]{:S(2)}) collective-permute-start(bf16[2048,128]{1,0:T(8,128)(2,1)S(1)} %get-tuple-element.20), channel_id=1, source_target_pairs={{0,8},{4,12},{8,0},{12,4},{16,24},{20,28},{24,16},{28,20},{1,9},{5... | collective-permute-start | bytes 1572872 | tf_op jit(solution)/shard_map/ppermute | solution.py:68
  5.6 15.6 %collective-permute-start.2 = (bf16[2048,128]{1,0:T(8,128)(2,1)S(1)}, bf16[2048,128]{1,0:T(8,128)(2,1)S(1)}, u32[]{:S(2)}, u32[]{:S(2)}) collective-permute-start(bf16[2048,128]{1,0:T(8,128)(2,1)S(1)} %get-tuple-element.21), channel_id=1, source_target_pairs={{0,16},{4,20},{8,24},{12,28},{16,0},{20,4},{24,8},{28,12},{1,17},{... | collective-permute-start | bytes 1572872 | tf_op jit(solution)/shard_map/ppermute | solution.py:68
  7.1 23.6 %collective-permute-start.3 = (bf16[2048,128]{1,0:T(8,128)(2,1)S(1)}, bf16[2048,128]{1,0:T(8,128)(2,1)S(1)}, u32[]{:S(2)}, u32[]{:S(2)}) collective-permute-start(bf16[2048,128]{1,0:T(8,128)(2,1)S(1)} %get-tuple-element.22), channel_id=1, source_target_pairs={{0,28},{4,24},{8,20},{12,16},{16,12},{20,8},{24,4},{28,0},{1,29},{... | collective-permute-start | bytes 1572872 | tf_op jit(solution)/shard_map/ppermute | solution.py:68
  7.1 32.2 %collective-permute-start.4 = (bf16[2048,128]{1,0:T(8,128)(2,1)S(1)}, bf16[2048,128]{1,0:T(8,128)(2,1)S(1)}, u32[]{:S(2)}, u32[]{:S(2)}) collective-permute-start(bf16[2048,128]{1,0:T(8,128)(2,1)S(1)} %get-tuple-element.23), channel_id=1, source_target_pairs={{0,12},{4,8},{8,4},{12,0},{16,28},{20,24},{24,20},{28,16},{1,13},{... | collective-permute-start | bytes 1572872 | tf_op jit(solution)/shard_map/ppermute | solution.py:68
  8.8 33.1 %collective-permute-start.5 = (bf16[2048,128]{1,0:T(8,128)(2,1)S(1)}, bf16[2048,128]{1,0:T(8,128)(2,1)S(1)}, u32[]{:S(2)}, u32[]{:S(2)}) collective-permute-start(bf16[2048,128]{1,0:T(8,128)(2,1)S(1)} %get-tuple-element.24), channel_id=1, source_target_pairs={{0,20},{4,16},{8,28},{12,24},{16,4},{20,0},{24,12},{28,8},{1,21},{... | collective-permute-start | bytes 1572872 | tf_op jit(solution)/shard_map/ppermute | solution.py:68
  10.2 72.9 %copy-start = (f32[128]{0:T(128)S(1)}, f32[128]{0:T(128)}, u32[]{:S(2)}) copy-start(f32[128]{0:T(128)} %param.7) | copy-start | bytes 1540
  19.1 23.4 %collective-permute-start.6 = (bf16[2048,128]{1,0:T(8,128)(2,1)S(1)}, bf16[2048,128]{1,0:T(8,128)(2,1)S(1)}, u32[]{:S(2)}, u32[]{:S(2)}) collective-permute-start(bf16[2048,128]{1,0:T(8,128)(2,1)S(1)} %get-tuple-element.25), channel_id=1, source_target_pairs={{0,4},{4,0},{8,12},{12,8},{16,20},{20,16},{24,28},{28,24},{1,5},{5... | collective-permute-start | bytes 1572872 | tf_op jit(solution)/shard_map/ppermute | solution.py:68
  21.2 32.5 %collective-permute-start = (bf16[2048,128]{1,0:T(8,128)(2,1)S(1)}, bf16[2048,128]{1,0:T(8,128)(2,1)S(1)}, u32[]{:S(2)}, u32[]{:S(2)}) collective-permute-start(bf16[2048,128]{1,0:T(8,128)(2,1)S(1)} %shard_map.67), channel_id=1, source_target_pairs={{0,24},{4,28},{8,16},{12,20},{16,8},{20,12},{24,0},{28,4},{1,25},{... | collective-permute-start | bytes 1572872 | tf_op jit(solution)/shard_map/ppermute | solution.py:68
  30.7 33.7 %collective-permute-start.10 = (bf16[2048,128]{1,0:T(8,128)(2,1)S(1)}, bf16[2048,128]{1,0:T(8,128)(2,1)S(1)}, u32[]{:S(2)}, u32[]{:S(2)}) collective-permute-start(bf16[2048,128]{1,0:T(8,128)(2,1)S(1)} %get-tuple-element.33), channel_id=1, source_target_pairs={{0,20},{4,16},{8,28},{12,24},{16,4},{20,0},{24,12},{28,8},{1,21},{... | collective-permute-start | bytes 1572872 | tf_op jit(solution)/shard_map/ppermute | solution.py:68
  39.3 25.2 %collective-permute-start.7 = (bf16[2048,128]{1,0:T(8,128)(2,1)S(1)}, bf16[2048,128]{1,0:T(8,128)(2,1)S(1)}, u32[]{:S(2)}, u32[]{:S(2)}) collective-permute-start(bf16[2048,128]{1,0:T(8,128)(2,1)S(1)} %get-tuple-element.30), channel_id=1, source_target_pairs={{0,4},{4,0},{8,12},{12,8},{16,20},{20,16},{24,28},{28,24},{1,5},{5... | collective-permute-start | bytes 1572872 | tf_op jit(solution)/shard_map/ppermute | solution.py:68
  41.9 60.2 %collective-permute-start.8 = (bf16[2048,128]{1,0:T(8,128)(2,1)S(1)}, bf16[2048,128]{1,0:T(8,128)(2,1)S(1)}, u32[]{:S(2)}, u32[]{:S(2)}) collective-permute-start(bf16[2048,128]{1,0:T(8,128)(2,1)S(1)} %get-tuple-element.31), channel_id=1, source_target_pairs={{0,16},{4,20},{8,24},{12,28},{16,0},{20,4},{24,8},{28,12},{1,17},{... | collective-permute-start | bytes 1572872 | tf_op jit(solution)/shard_map/ppermute | solution.py:68
  42.5 59.7 %collective-permute-start.9 = (bf16[2048,128]{1,0:T(8,128)(2,1)S(1)}, bf16[2048,128]{1,0:T(8,128)(2,1)S(1)}, u32[]{:S(2)}, u32[]{:S(2)}) collective-permute-start(bf16[2048,128]{1,0:T(8,128)(2,1)S(1)} %get-tuple-element.32), channel_id=1, source_target_pairs={{0,8},{4,12},{8,0},{12,4},{16,24},{20,28},{24,16},{28,20},{1,9},{5... | collective-permute-start | bytes 1572872 | tf_op jit(solution)/shard_map/ppermute | solution.py:68
  53.7 50.8 %collective-permute-start.11 = (bf16[2048,128]{1,0:T(8,128)(2,1)S(1)}, bf16[2048,128]{1,0:T(8,128)(2,1)S(1)}, u32[]{:S(2)}, u32[]{:S(2)}) collective-permute-start(bf16[2048,128]{1,0:T(8,128)(2,1)S(1)} %get-tuple-element.34), channel_id=1, source_target_pairs={{0,12},{4,8},{8,4},{12,0},{16,28},{20,24},{24,20},{28,16},{1,13},{... | collective-permute-start | bytes 1572872 | tf_op jit(solution)/shard_map/ppermute | solution.py:68
  64.4 40.9 %collective-permute-start.12 = (bf16[2048,128]{1,0:T(8,128)(2,1)S(1)}, bf16[2048,128]{1,0:T(8,128)(2,1)S(1)}, u32[]{:S(2)}, u32[]{:S(2)}) collective-permute-start(bf16[2048,128]{1,0:T(8,128)(2,1)S(1)} %get-tuple-element.35), channel_id=1, source_target_pairs={{0,24},{4,28},{8,16},{12,20},{16,8},{20,12},{24,0},{28,4},{1,25},{... | collective-permute-start | bytes 1572872 | tf_op jit(solution)/shard_map/ppermute | solution.py:68
  64.5 41.7 %collective-permute-start.13 = (bf16[2048,128]{1,0:T(8,128)(2,1)S(1)}, bf16[2048,128]{1,0:T(8,128)(2,1)S(1)}, u32[]{:S(2)}, u32[]{:S(2)}) collective-permute-start(bf16[2048,128]{1,0:T(8,128)(2,1)S(1)} %get-tuple-element.36), channel_id=1, source_target_pairs={{0,28},{4,24},{8,20},{12,16},{16,12},{20,8},{24,4},{28,0},{1,29},{... | collective-permute-start | bytes 1572872 | tf_op jit(solution)/shard_map/ppermute | solution.py:68

commit v2 on v1

v2 whole, which is shorter than its diff:
```python
import functools

import jax
import jax.numpy as jnp
from jax import lax
from jax.experimental import pallas as pl
from jax.experimental.pallas import tpu as pltpu
from jax.sharding import PartitionSpec as P


GROUP = ("farcp", "nearcp")
TILE = 128
UNROLL = 2
PARTS = 2


def partner(me, step, count):
    return me ^ step if count & (count - 1) == 0 else (me + step) % count


def sender(me, step, count):
    return me ^ step if count & (count - 1) == 0 else (me + count - step) % count


def orders(count):
    def hops(step):
        return bin(step >> 1).count("1")

    steps = range(1, count)
    keys = sorted(steps, key=lambda step: (step < 2, step & 1, -hops(step), step))
    values = sorted(steps, key=lambda step: (hops(step), step & 1, -step))
    return tuple(keys), tuple(values)


def in_hbm(array):
    return pltpu.with_memory_space_constraint(array, pltpu.HBM)


def cut_kernel(count, steps, whole, *refs):
    pieces, sems = refs[: len(steps)], refs[len(steps)]
    me = lax.axis_index(GROUP)
    copies = [
        pltpu.make_async_copy(whole.at[partner(me, step, count)], piece, sems.at[slot])
        for slot, (step, piece) in enumerate(zip(steps, pieces))
    ]
    for copy in copies:
        copy.start()
    for copy in copies:
        copy.wait()


def cut(whole, steps):
    count, rows, lanes = whole.shape
    return pl.pallas_call(
        functools.partial(cut_kernel, count, steps),
        out_shape=[pltpu.VMEM((rows, lanes), whole.dtype)] * len(steps),
        in_specs=[pl.BlockSpec(memory_space=pltpu.HBM)],
        out_specs=[pl.BlockSpec(memory_space=pltpu.VMEM)] * len(steps),
        scratch_shapes=[pltpu.SemaphoreType.DMA((len(steps),))],
        compiler_params=pltpu.CompilerParams(vmem_limit_bytes=8 << 20),
    )(in_hbm(whole))


def exchange(pieces, steps, count):
    moved = []
    for step, piece in zip(steps, pieces):
        pairs = [(source, int(partner(source, step, count))) for source in range(count)]
        moved.append(lax.ppermute(piece, GROUP, pairs))
    return moved


def table_kernel(heads, angle, cosine, sine):
    turn = angle[...]
    c, s = jnp.cos(turn), jnp.sin(turn)
    c = jnp.concatenate([c, c], axis=0).T
    s = jnp.concatenate([-s, s], axis=0).T
    for head in range(heads):
        at = pl.ds(head, c.shape[0], stride=heads)
        cosine[at, :] = c
        sine[at, :] = s


def tables(turn_angle, heads, block=512):
    length, half = turn_angle.shape
    shape = pltpu.VMEM((length * heads, 2 * half), jnp.float32)
    return pl.pallas_call(
        functools.partial(table_kernel, heads),
        out_shape=[shape, shape],
        grid=(length // block,),
        in_specs=[pl.BlockSpec((half, block), lambda i: (0, i))],
        out_specs=[pl.BlockSpec((block * heads, 2 * half), lambda i: (i, 0))] * 2,
        compiler_params=pltpu.CompilerParams(vmem_limit_bytes=8 << 20),
        cost_estimate=pl.CostEstimate(flops=length * half * 400, bytes_accessed=length * half * 40, transcendentals=0),
    )(in_hbm(turn_angle.T))


def keys_kernel(count, heads, steps, *refs):
    number = len(steps)
    pieces = refs[:number]
    cosine, sine, gain, stored, scale, turned, out, out_sems = refs[number:]
    rows, lanes = pieces[0].shape
    half = lanes // 2
    me = lax.axis_index(GROUP)
    starts = [pl.multiple_of(sender(me, step, count) * rows, rows) for step in steps]
    peak = jnp.zeros((8, lanes), jnp.float32)
    factor = gain[...]
    for slot, piece in enumerate(pieces):

        def turn(index, peak, slot=slot, piece=piece):
            part = pl.ds(pl.multiple_of(index * TILE, TILE), TILE)
            place = pl.ds(pl.multiple_of(starts[slot] + index * TILE, TILE), TILE)
            wide = piece[part, :].astype(jnp.float32)
            mean = jnp.sum(wide * wide, axis=-1, keepdims=True) * (1.0 / lanes)
            wide = wide * lax.rsqrt(mean + 1e-06) * factor
            wide = wide * cosine[place, :] + pltpu.roll(wide, half, 1) * sine[place, :]
            turned[slot, part, :] = wide
            return jnp.maximum(peak, jnp.max(jnp.abs(wide).reshape(TILE // 8, 8, lanes), axis=0))

        peak = lax.fori_loop(0, rows // TILE, turn, peak, unroll=UNROLL)
    tops = [peak[head : head + 1] for head in range(heads)]
    for row in range(heads, 8):
        tops[row % heads] = jnp.maximum(tops[row % heads], peak[row : row + 1])
    top = jnp.concatenate(tops, axis=0)
    scale[...] = top
    inverse = 1.0 / jnp.concatenate([top] * (8 // heads), axis=0)
    copies = [
        pltpu.make_async_copy(out.at[slot % 2], stored.at[pl.ds(starts[slot], rows)], out_sems.at[slot % 2])
        for slot in range(number)
    ]
    for slot in range(number):
        if slot >= 2:
            copies[slot - 2].wait()

        def narrow(index, carry, slot=slot):
            part = pl.ds(pl.multiple_of(index * TILE, TILE), TILE)
            wide = turned[slot, part, :].reshape(TILE // 8, 8, lanes) * inverse[None]
            out[slot % 2, part, :] = wide.reshape(TILE, lanes).astype(out.dtype)
            return carry

        lax.fori_loop(0, rows // TILE, narrow, 0, unroll=UNROLL)
        copies[slot].start()
    for copy in copies[-2:]:
        copy.wait()


def finish_keys(pieces, cosine, sine, gain, steps, heads):
    count = len(steps)
    rows, lanes = pieces[0].shape
    dtype = pieces[0].dtype
    return pl.pallas_call(
        functools.partial(keys_kernel, count, heads, steps),
        out_shape=[
            pltpu.HBM((count * rows, lanes), dtype),
            jax.ShapeDtypeStruct((heads, lanes), jnp.float32),
        ],
        in_specs=[pl.BlockSpec(memory_space=pltpu.VMEM)] * (len(pieces) + 3),
        out_specs=[pl.BlockSpec(memory_space=pltpu.HBM), pl.BlockSpec(memory_space=pltpu.VMEM)],
        scratch_shapes=[
            pltpu.VMEM((count, rows, lanes), jnp.float32),
            pltpu.VMEM((2, rows, lanes), dtype),
            pltpu.SemaphoreType.DMA((2,)),
        ],
        compiler_params=pltpu.CompilerParams(vmem_limit_bytes=16 << 20),
        cost_estimate=pl.CostEstimate(flops=count * rows * lanes * 200, bytes_accessed=count * rows * lanes * 8, transcendentals=0),
    )(*pieces, cosine, sine, gain)


def place_kernel(count, steps, before, *refs):
    del before
    number = len(steps)
    pieces, whole, sems = refs[:number], refs[number], refs[number + 1]
    rows = whole.shape[0] // count
    me = lax.axis_index(GROUP)
    size = rows // PARTS
    copies = [
        pltpu.make_async_copy(
            piece.at[pl.ds(part * size, size)],
            whole.at[pl.ds(sender(me, step, count) * rows + part * size, size)],
            sems.at[slot, part],
        )
        for slot, (step, piece) in enumerate(zip(steps, pieces))
        for part in range(PARTS)
    ]
    for copy in copies:
        copy.start()
    for copy in copies:
        copy.wait()


def place(before, pieces, steps, count):
    rows, lanes = pieces[0].shape
    number = len(steps)
    whole = pltpu.HBM((count * rows, lanes), pieces[0].dtype)
    return pl.pallas_call(
        functools.partial(place_kernel, count, steps),
        out_shape=whole,
        in_specs=[pl.BlockSpec(memory_space=pltpu.HBM)] + [pl.BlockSpec(memory_space=pltpu.VMEM)] * number,
        out_specs=pl.BlockSpec(memory_space=pltpu.HBM),
        scratch_shapes=[pltpu.SemaphoreType.DMA((number, PARTS))],
        input_output_aliases={0: 0} if before.shape == whole.shape else {},
        compiler_params=pltpu.CompilerParams(vmem_limit_bytes=4 << 20),
    )(in_hbm(before), *pieces)


def local(raw_keys, raw_values, turn_angle, key_gain):
    count, length, heads, lanes = raw_keys.shape
    rows = length * heads
    keys = raw_keys.reshape(count, rows, lanes)
    values = raw_values.reshape(count, rows, lanes)
    steps, value_steps = orders(count)
    early = cut(keys, steps[:1])
    early = [*early, *cut(keys, steps[1:] + (0,))]
    late = cut(values, value_steps + (0,))
    key_pieces = exchange(early[:-1], steps, count) + [early[-1]]
    value_pieces = exchange(late[:-1], value_steps, count)
    cosine, sine = tables(turn_angle, heads)
    stored_keys, key_scale = finish_keys(key_pieces, cosine, sine, key_gain.reshape(1, lanes), steps + (0,), heads)
    arrived = {0: late[-1], **dict(zip(value_steps, value_pieces))}
    stored_values = key_scale
    for group in ((0,) + value_steps[:-3], value_steps[-3:-2], value_steps[-2:-1], value_steps[-1:]):
        if group:
            stored_values = place(stored_values, [arrived[step] for step in group], group, count)
    whole = (1, count * length, heads, lanes)
    return stored_keys.reshape(whole), stored_values.reshape(whole), key_scale[None]


def solution(mesh):
    in_specs = (
        P(None, GROUP, "model", None),
        P(None, GROUP, "model", None),
        P(),
        P(),
    )
    out_specs = (
        P(GROUP, None, "model", None),
        P(GROUP, None, "model", None),
        P(GROUP, "model", None),
    )
    return jax.shard_map(local, mesh=mesh, in_specs=in_specs, out_specs=out_specs, check_vma=False)
```

time: 108 us -> 103 us (0.954)
  Pallas kernels: 44.1 us -> 39.6 us
    pallas_call x1, Pallas kernels: 15.3 us -> 12.9 us  [tables(): pl.pallas_call(functools.partial(table_kernel, heads), out_shape=[shape,...]
    pallas_call x1, Pallas kernels: 19 us -> 17.3 us  [finish_keys(): pl.pallas_call(functools.partial(keys_kernel, count, heads, steps), out_s...]
  transfers between devices with their start and end apart: 14 -> 14, of which waited for: 6 -> 6; matrix products, arithmetic and copies ran while one was open for 0% -> 0% of each run, Pallas kernels for 39% -> 36%
where the time goes in v2:
time: 103 us; the launch traced here: 102 us
  waiting for transfers between devices  44.3 us (43%)
  Pallas kernels  39.6 us (38%)
  starting transfers between devices  17.6 us (17%)
    ppermute x14, waiting for transfers between devices, exchange(): moved.append(lax.ppermute(piece, GROUP, pairs))  44.3 us
    ppermute x14, starting transfers between devices, exchange(): moved.append(lax.ppermute(piece, GROUP, pairs))  17.6 us
    pallas_call x1, Pallas kernels, finish_keys(): pl.pallas_call(functools.partial(keys_kernel, count, heads, steps), out_s...  17.3 us
    pallas_call x1, Pallas kernels, tables(): pl.pallas_call(functools.partial(table_kernel, heads), out_shape=[shape,...  12.9 us
    pallas_call x3, Pallas kernels, cut(): pl.pallas_call(functools.partial(cut_kernel, count, steps), out_shape=[pl...  5.33 us
    pallas_call x4, Pallas kernels, place(): pl.pallas_call(functools.partial(place_kernel, count, steps), out_shape=w...  4.05 us
  transfers between devices with their start and end apart: 14, of which 6 were waited for; matrix products, arithmetic and copies ran while one was open for 0% of the time, Pallas kernels for 36%

profile of v2, /device:TPU:0, one launch (start us, length us, event | category | flops | bytes accessed | tf_op | source)
XLA Modules:
  0.0 102.3 jit_solution(8815082421113244586)
XLA Ops:
  0.6 2.1 %shard_map.68 = (bf16[2048,128]{1,0:T(8,128)(2,1)S(1)}, bf16[2048,128]{1,0:T(8,128)(2,1)S(1)}, bf16[2048,128]{1,0:T(8,128)(2,1)S(1)}, bf16[2048,128]{1,0:T(8,128...) custom-call(bf16[8,2048,128]{2,1,0:T(8,128)(2,1)} %bitcast.9), custom_call_target="tpu_custom_call" | custom-call | tf_op jit(solution)/shard_map/pallas_call | solution.py:54
  2.7 3.1 %collective-permute-start.1 = (bf16[2048,128]{1,0:T(8,128)(2,1)S(1)}, bf16[2048,128]{1,0:T(8,128)(2,1)S(1)}, u32[]{:S(2)}, u32[]{:S(2)}) collective-permute-start(bf16[2048,128]{1,0:T(8,128)(2,1)S(1)} %get-tuple-element.22), channel_id=1, source_target_pairs={{0,8},{4,12},{8,0},{12,4},{16,24},{20,28},{24,16},{28,20},{1,9},{5... | collective-permute-start | bytes 1572872 | tf_op jit(solution)/shard_map/ppermute | solution.py:68
  5.8 1.5 %collective-permute-start.2 = (bf16[2048,128]{1,0:T(8,128)(2,1)S(1)}, bf16[2048,128]{1,0:T(8,128)(2,1)S(1)}, u32[]{:S(2)}, u32[]{:S(2)}) collective-permute-start(bf16[2048,128]{1,0:T(8,128)(2,1)S(1)} %get-tuple-element.23), channel_id=1, source_target_pairs={{0,16},{4,20},{8,24},{12,28},{16,0},{20,4},{24,8},{28,12},{1,17},{... | collective-permute-start | bytes 1572872 | tf_op jit(solution)/shard_map/ppermute | solution.py:68
  7.3 1.7 %collective-permute-start.4 = (bf16[2048,128]{1,0:T(8,128)(2,1)S(1)}, bf16[2048,128]{1,0:T(8,128)(2,1)S(1)}, u32[]{:S(2)}, u32[]{:S(2)}) collective-permute-start(bf16[2048,128]{1,0:T(8,128)(2,1)S(1)} %get-tuple-element.25), channel_id=1, source_target_pairs={{0,12},{4,8},{8,4},{12,0},{16,28},{20,24},{24,20},{28,16},{1,13},{... | collective-permute-start | bytes 1572872 | tf_op jit(solution)/shard_map/ppermute | solution.py:68
  9.3 1.0 %shard_map.67 = bf16[2048,128]{1,0:T(8,128)(2,1)S(1)} custom-call(bf16[8,2048,128]{2,1,0:T(8,128)(2,1)} %bitcast.10), custom_call_target="tpu_custom_call" | custom-call | tf_op jit(solution)/shard_map/pallas_call | solution.py:54
  10.4 8.8 %collective-permute-done.1.refs_1_ = bf16[2048,128]{1,0:T(8,128)(2,1)S(1)} collective-permute-done((bf16[2048,128]{1,0:T(8,128)(2,1)S(1)}, bf16[2048,128]{1,0:T(8,128)(2,1)S(1)}, u32[]{:S(2)}, u32[]{:S(2)}) %collective-permute-start.1) | collective-permute-done | bytes 524320 | tf_op jit(solution)/shard_map/ppermute | solution.py:68
  19.3 2.2 %shard_map.71 = (bf16[2048,128]{1,0:T(8,128)(2,1)S(1)}, bf16[2048,128]{1,0:T(8,128)(2,1)S(1)}, bf16[2048,128]{1,0:T(8,128)(2,1)S(1)}, bf16[2048,128]{1,0:T(8,128...) custom-call(bf16[8,2048,128]{2,1,0:T(8,128)(2,1)} %bitcast.11), custom_call_target="tpu_custom_call" | custom-call | tf_op jit(solution)/shard_map/pallas_call | solution.py:54
  21.5 3.6 %collective-permute-start = (bf16[2048,128]{1,0:T(8,128)(2,1)S(1)}, bf16[2048,128]{1,0:T(8,128)(2,1)S(1)}, u32[]{:S(2)}, u32[]{:S(2)}) collective-permute-start(bf16[2048,128]{1,0:T(8,128)(2,1)S(1)} %shard_map.67), channel_id=1, source_target_pairs={{0,24},{4,28},{8,16},{12,20},{16,8},{20,12},{24,0},{28,4},{1,25},{... | collective-permute-start | bytes 1572872 | tf_op jit(solution)/shard_map/ppermute | solution.py:68
  25.1 5.7 %collective-permute-done.3.refs_3_ = bf16[2048,128]{1,0:T(8,128)(2,1)S(1)} collective-permute-done((bf16[2048,128]{1,0:T(8,128)(2,1)S(1)}, bf16[2048,128]{1,0:T(8,128)(2,1)S(1)}, u32[]{:S(2)}, u32[]{:S(2)}) %collective-permute-start.3) | collective-permute-done | bytes 524320 | tf_op jit(solution)/shard_map/ppermute | solution.py:68
  30.8 1.9 %collective-permute-start.10 = (bf16[2048,128]{1,0:T(8,128)(2,1)S(1)}, bf16[2048,128]{1,0:T(8,128)(2,1)S(1)}, u32[]{:S(2)}, u32[]{:S(2)}) collective-permute-start(bf16[2048,128]{1,0:T(8,128)(2,1)S(1)} %get-tuple-element.37), channel_id=1, source_target_pairs={{0,20},{4,16},{8,28},{12,24},{16,4},{20,0},{24,12},{28,8},{1,21},{... | collective-permute-start | bytes 1572872 | tf_op jit(solution)/shard_map/ppermute | solution.py:68
  32.7 6.8 %collective-permute-done.4.refs_4_ = bf16[2048,128]{1,0:T(8,128)(2,1)S(1)} collective-permute-done((bf16[2048,128]{1,0:T(8,128)(2,1)S(1)}, bf16[2048,128]{1,0:T(8,128)(2,1)S(1)}, u32[]{:S(2)}, u32[]{:S(2)}) %collective-permute-start.4) | collective-permute-done | bytes 524320 | tf_op jit(solution)/shard_map/ppermute | solution.py:68
  39.5 0.8 collective-permute-start.7
  40.3 1.8 %collective-permute-done.5.refs_5_ = bf16[2048,128]{1,0:T(8,128)(2,1)S(1)} collective-permute-done((bf16[2048,128]{1,0:T(8,128)(2,1)S(1)}, bf16[2048,128]{1,0:T(8,128)(2,1)S(1)}, u32[]{:S(2)}, u32[]{:S(2)}) %collective-permute-start.5) | collective-permute-done | bytes 524320 | tf_op jit(solution)/shard_map/ppermute | solution.py:68
  42.1 0.5 collective-permute-start.8
  42.6 0.8 collective-permute-start.9
  43.4 10.5 %collective-permute-done.refs_0_ = bf16[2048,128]{1,0:T(8,128)(2,1)S(1)} collective-permute-done((bf16[2048,128]{1,0:T(8,128)(2,1)S(1)}, bf16[2048,128]{1,0:T(8,128)(2,1)S(1)}, u32[]{:S(2)}, u32[]{:S(2)}) %collective-permute-start) | collective-permute-done | bytes 524320 | tf_op jit(solution)/shard_map/ppermute | solution.py:68
  53.9 10.7 %collective-permute-done.10.refs_4_ = bf16[2048,128]{1,0:T(8,128)(2,1)S(1)} collective-permute-done((bf16[2048,128]{1,0:T(8,128)(2,1)S(1)}, bf16[2048,128]{1,0:T(8,128)(2,1)S(1)}, u32[]{:S(2)}, u32[]{:S(2)}) %collective-permute-start.10) | collective-permute-done | bytes 524320 | tf_op jit(solution)/shard_map/ppermute | solution.py:68
  64.6 3.3 %collective-permute-start.13 = (bf16[2048,128]{1,0:T(8,128)(2,1)S(1)}, bf16[2048,128]{1,0:T(8,128)(2,1)S(1)}, u32[]{:S(2)}, u32[]{:S(2)}) collective-permute-start(bf16[2048,128]{1,0:T(8,128)(2,1)S(1)} %get-tuple-element.40), channel_id=1, source_target_pairs={{0,28},{4,24},{8,20},{12,16},{16,12},{20,8},{24,4},{28,0},{1,29},{... | collective-permute-start | bytes 1572872 | tf_op jit(solution)/shard_map/ppermute | solution.py:68
  68.0 12.9 %shard_map.69 = (f32[16384,128]{1,0:T(8,128)S(1)}, f32[16384,128]{1,0:T(8,128)S(1)}) custom-call(f32[64,8192]{1,0:T(8,128)} %bitcast.12), custom_call_target="tpu_custom_call" | custom-call | flops 209715200 | bytes 20971520 | tf_op jit(solution)/shard_map/pallas_call | solution.py:86
  80.9 17.3 %shard_map.70 = (bf16[16384,128]{1,0:T(8,128)(2,1)}, f32[2,128]{1,0:T(2,128)}) custom-call(bf16[2048,128]{1,0:T(8,128)(2,1)S(1)} %collective-permute-done.refs_0_, bf16[2048,128]{1,0:T(8,128)(2,1)S(1)} %collective-permute-done.1.refs_1_, bf16[2048,128]{1,0:T(8,128)(2,1)S(1)} %collective-permute-done.2.refs_2_, ...), custom_call_target="tpu_custom_call" | custom-call | flops 419430400 | bytes 16777216 | tf_op jit(solution)/shard_map/pallas_call | solution.py:150
  98.2 1.6 %shard_map.72.before = bf16[16384,128]{1,0:T(8,128)(2,1)} custom-call(f32[2,128]{1,0:T(2,128)} %get-tuple-element.32.before, bf16[2048,128]{1,0:T(8,128)(2,1)S(1)} %get-tuple-element.33.refs_0_, bf16[2048,128]{1,0:T(8,128)(2,1)S(1)} %collective-permute-done.7.refs_1_, bf16[2048,128]{1,0:T(8,128)(2,1)S(1)} %collective-permute-done.8.refs_2_, ...), custom_call_target="tpu_custom_call" | custom-call | tf_op jit(solution)/shard_map/pallas_call | solution.py:194
  99.8 0.8 shard_map.73.before
  100.7 0.8 shard_map.74.before
  101.5 0.8 shard_map.75
  (15 shorter events, 0.5 us)
Async XLA Ops:
  2.7 16.6 %collective-permute-start.1 = (bf16[2048,128]{1,0:T(8,128)(2,1)S(1)}, bf16[2048,128]{1,0:T(8,128)(2,1)S(1)}, u32[]{:S(2)}, u32[]{:S(2)}) collective-permute-start(bf16[2048,128]{1,0:T(8,128)(2,1)S(1)} %get-tuple-element.22), channel_id=1, source_target_pairs={{0,8},{4,12},{8,0},{12,4},{16,24},{20,28},{24,16},{28,20},{1,9},{5... | collective-permute-start | bytes 1572872 | tf_op jit(solution)/shard_map/ppermute | solution.py:68
  5.8 15.7 %collective-permute-start.2 = (bf16[2048,128]{1,0:T(8,128)(2,1)S(1)}, bf16[2048,128]{1,0:T(8,128)(2,1)S(1)}, u32[]{:S(2)}, u32[]{:S(2)}) collective-permute-start(bf16[2048,128]{1,0:T(8,128)(2,1)S(1)} %get-tuple-element.23), channel_id=1, source_target_pairs={{0,16},{4,20},{8,24},{12,28},{16,0},{20,4},{24,8},{28,12},{1,17},{... | collective-permute-start | bytes 1572872 | tf_op jit(solution)/shard_map/ppermute | solution.py:68
  7.3 23.6 %collective-permute-start.3 = (bf16[2048,128]{1,0:T(8,128)(2,1)S(1)}, bf16[2048,128]{1,0:T(8,128)(2,1)S(1)}, u32[]{:S(2)}, u32[]{:S(2)}) collective-permute-start(bf16[2048,128]{1,0:T(8,128)(2,1)S(1)} %get-tuple-element.24), channel_id=1, source_target_pairs={{0,28},{4,24},{8,20},{12,16},{16,12},{20,8},{24,4},{28,0},{1,29},{... | collective-permute-start | bytes 1572872 | tf_op jit(solution)/shard_map/ppermute | solution.py:68
  7.3 32.2 %collective-permute-start.4 = (bf16[2048,128]{1,0:T(8,128)(2,1)S(1)}, bf16[2048,128]{1,0:T(8,128)(2,1)S(1)}, u32[]{:S(2)}, u32[]{:S(2)}) collective-permute-start(bf16[2048,128]{1,0:T(8,128)(2,1)S(1)} %get-tuple-element.25), channel_id=1, source_target_pairs={{0,12},{4,8},{8,4},{12,0},{16,28},{20,24},{24,20},{28,16},{1,13},{... | collective-permute-start | bytes 1572872 | tf_op jit(solution)/shard_map/ppermute | solution.py:68
  9.0 33.1 %collective-permute-start.5 = (bf16[2048,128]{1,0:T(8,128)(2,1)S(1)}, bf16[2048,128]{1,0:T(8,128)(2,1)S(1)}, u32[]{:S(2)}, u32[]{:S(2)}) collective-permute-start(bf16[2048,128]{1,0:T(8,128)(2,1)S(1)} %get-tuple-element.26), channel_id=1, source_target_pairs={{0,20},{4,16},{8,28},{12,24},{16,4},{20,0},{24,12},{28,8},{1,21},{... | collective-permute-start | bytes 1572872 | tf_op jit(solution)/shard_map/ppermute | solution.py:68
  10.4 70.5 %copy-start = (f32[128]{0:T(128)S(1)}, f32[128]{0:T(128)}, u32[]{:S(2)}) copy-start(f32[128]{0:T(128)} %param.7) | copy-start | bytes 1540
  19.3 23.4 %collective-permute-start.6 = (bf16[2048,128]{1,0:T(8,128)(2,1)S(1)}, bf16[2048,128]{1,0:T(8,128)(2,1)S(1)}, u32[]{:S(2)}, u32[]{:S(2)}) collective-permute-start(bf16[2048,128]{1,0:T(8,128)(2,1)S(1)} %get-tuple-element.27), channel_id=1, source_target_pairs={{0,4},{4,0},{8,12},{12,8},{16,20},{20,16},{24,28},{28,24},{1,5},{5... | collective-permute-start | bytes 1572872 | tf_op jit(solution)/shard_map/ppermute | solution.py:68
  21.5 32.4 %collective-permute-start = (bf16[2048,128]{1,0:T(8,128)(2,1)S(1)}, bf16[2048,128]{1,0:T(8,128)(2,1)S(1)}, u32[]{:S(2)}, u32[]{:S(2)}) collective-permute-start(bf16[2048,128]{1,0:T(8,128)(2,1)S(1)} %shard_map.67), channel_id=1, source_target_pairs={{0,24},{4,28},{8,16},{12,20},{16,8},{20,12},{24,0},{28,4},{1,25},{... | collective-permute-start | bytes 1572872 | tf_op jit(solution)/shard_map/ppermute | solution.py:68
  30.8 33.7 %collective-permute-start.10 = (bf16[2048,128]{1,0:T(8,128)(2,1)S(1)}, bf16[2048,128]{1,0:T(8,128)(2,1)S(1)}, u32[]{:S(2)}, u32[]{:S(2)}) collective-permute-start(bf16[2048,128]{1,0:T(8,128)(2,1)S(1)} %get-tuple-element.37), channel_id=1, source_target_pairs={{0,20},{4,16},{8,28},{12,24},{16,4},{20,0},{24,12},{28,8},{1,21},{... | collective-permute-start | bytes 1572872 | tf_op jit(solution)/shard_map/ppermute | solution.py:68
  39.5 25.2 %collective-permute-start.7 = (bf16[2048,128]{1,0:T(8,128)(2,1)S(1)}, bf16[2048,128]{1,0:T(8,128)(2,1)S(1)}, u32[]{:S(2)}, u32[]{:S(2)}) collective-permute-start(bf16[2048,128]{1,0:T(8,128)(2,1)S(1)} %get-tuple-element.34), channel_id=1, source_target_pairs={{0,4},{4,0},{8,12},{12,8},{16,20},{20,16},{24,28},{28,24},{1,5},{5... | collective-permute-start | bytes 1572872 | tf_op jit(solution)/shard_map/ppermute | solution.py:68
  42.1 56.1 %collective-permute-start.8 = (bf16[2048,128]{1,0:T(8,128)(2,1)S(1)}, bf16[2048,128]{1,0:T(8,128)(2,1)S(1)}, u32[]{:S(2)}, u32[]{:S(2)}) collective-permute-start(bf16[2048,128]{1,0:T(8,128)(2,1)S(1)} %get-tuple-element.35), channel_id=1, source_target_pairs={{0,16},{4,20},{8,24},{12,28},{16,0},{20,4},{24,8},{28,12},{1,17},{... | collective-permute-start | bytes 1572872 | tf_op jit(solution)/shard_map/ppermute | solution.py:68
  42.6 55.6 %collective-permute-start.9 = (bf16[2048,128]{1,0:T(8,128)(2,1)S(1)}, bf16[2048,128]{1,0:T(8,128)(2,1)S(1)}, u32[]{:S(2)}, u32[]{:S(2)}) collective-permute-start(bf16[2048,128]{1,0:T(8,128)(2,1)S(1)} %get-tuple-element.36), channel_id=1, source_target_pairs={{0,8},{4,12},{8,0},{12,4},{16,24},{20,28},{24,16},{28,20},{1,9},{5... | collective-permute-start | bytes 1572872 | tf_op jit(solution)/shard_map/ppermute | solution.py:68
  53.9 46.0 %collective-permute-start.11 = (bf16[2048,128]{1,0:T(8,128)(2,1)S(1)}, bf16[2048,128]{1,0:T(8,128)(2,1)S(1)}, u32[]{:S(2)}, u32[]{:S(2)}) collective-permute-start(bf16[2048,128]{1,0:T(8,128)(2,1)S(1)} %get-tuple-element.38), channel_id=1, source_target_pairs={{0,12},{4,8},{8,4},{12,0},{16,28},{20,24},{24,20},{28,16},{1,13},{... | collective-permute-start | bytes 1572872 | tf_op jit(solution)/shard_map/ppermute | solution.py:68
  64.6 36.1 %collective-permute-start.12 = (bf16[2048,128]{1,0:T(8,128)(2,1)S(1)}, bf16[2048,128]{1,0:T(8,128)(2,1)S(1)}, u32[]{:S(2)}, u32[]{:S(2)}) collective-permute-start(bf16[2048,128]{1,0:T(8,128)(2,1)S(1)} %get-tuple-element.39), channel_id=1, source_target_pairs={{0,24},{4,28},{8,16},{12,20},{16,8},{20,12},{24,0},{28,4},{1,25},{... | collective-permute-start | bytes 1572872 | tf_op jit(solution)/shard_map/ppermute | solution.py:68
  64.6 36.9 %collective-permute-start.13 = (bf16[2048,128]{1,0:T(8,128)(2,1)S(1)}, bf16[2048,128]{1,0:T(8,128)(2,1)S(1)}, u32[]{:S(2)}, u32[]{:S(2)}) collective-permute-start(bf16[2048,128]{1,0:T(8,128)(2,1)S(1)} %get-tuple-element.40), channel_id=1, source_target_pairs={{0,28},{4,24},{8,20},{12,16},{16,12},{20,8},{24,4},{28,0},{1,29},{... | collective-permute-start | bytes 1572872 | tf_op jit(solution)/shard_map/ppermute | solution.py:68
